TPU v7x, 32 devices: a whole 2x2x4 slice. The times are simulated.
32 devices in a mesh: dp: 8 (over z, y), mp: 4 (over x, core).
Axes of the slice: x: 2, y: 2, z: 4, core: 2. Of those that a mesh axis runs over, the one named last changes fastest.
Arguments:
- features: bfloat16 [3, 512, 16384], P(None, 'mp', 'dp'), may hold values from -6 to 6
- weights: bfloat16 [11, 512, 512], P(None, 'mp'), may hold values from -0.25 to 0.25
- sample_owner: int32 [3, 16384, 1], P(None, 'dp'), may hold values from 0 to 7; in each aligned block of 2048 rows (0 to 2047, 2048 to 4095, ..., all dimensions but the last counted through in order) at most 512 rows name the same one
- sample_row: int32 [3, 16384], P(None, 'dp'), may hold values from 0 to 2047
- edge_src: int32 [8, 16384], P(None, 'dp'), may hold values from 0 to 2047
- edge_dst: int32 [8, 16384], P(None, 'dp'), may hold values from 0 to 127
- edge_count: int32 [8, 8], P(None, 'dp'), may hold values from 128 to 2048
Outputs:
- updated: bfloat16 [3, 512, 1024], P(None, 'mp', 'dp')
Inputs may be any that keep to these rules, and one draw needn't show every extreme that they name: `sample_owner`: among the 2048 entries of one node type in one block no owner appears more than 512 times; some owner appears exactly 512 times in some blocks.
All inputs are finite; a program needn't handle non-finite values.
Results may differ from a plain program's by a relative error of at most 0.0064.
Values may be sent and summed in bfloat16 or wider, within the bound.
A program may use at most 64 MiB of HBM per device.

v0:
```python
import math
import jax
import jax.numpy as jnp
from jax import lax
from jax.sharding import PartitionSpec as P

RELS = 8
SEEDS = 128
RELATION_SOURCE = (0, 1, 0, 1, 2, 0, 2, 1)
MATRIX_TARGET = (1, 0, 0, 2, 1, 2, 0, 1, 0, 1, 2)


def pick_columns(table, index):
    count = index.shape[0]
    block_size = math.gcd(count, 512)
    row_ids = jnp.arange(table.shape[1], dtype=jnp.int32)[:, None]

    def one_block(block):
        chosen = (row_ids == block[None, :]).astype(jnp.bfloat16)
        return jnp.dot(table, chosen, preferred_element_type=jnp.float32).astype(jnp.bfloat16)

    picked = lax.map(one_block, index.reshape(count // block_size, block_size))
    return picked.transpose(1, 0, 2).reshape(table.shape[0], count)


def serve_kind(kind_table, requested):
    picked = pick_columns(kind_table, requested.reshape(-1))
    picked = picked.reshape(kind_table.shape[0], requested.shape[0], requested.shape[1])
    return lax.all_to_all(picked, "dp", split_axis=1, concat_axis=1, tiled=True)


def contract_first(left, right):
    return lax.dot_general(
        left, right, (((0,), (0,)), ((), ())), preferred_element_type=jnp.float32
    )


def per_device(features, weights, sample_owner, sample_row, edge_src, edge_dst, edge_count):
    groups = lax.axis_size("dp")
    node_kinds = features.shape[0]
    width_here = features.shape[1]
    sampled = sample_row.shape[1]
    capacity = 2 * sampled // groups
    owners = sample_owner[:, :, 0]
    owner_hot = (owners[:, :, None] == jnp.arange(groups, dtype=jnp.int32)[None, None, :]).astype(
        jnp.float32
    )
    block_size = math.gcd(sampled, 512)
    blocks = owner_hot.reshape(node_kinds, sampled // block_size, block_size, groups)
    block_ids = jnp.arange(block_size, dtype=jnp.int32)
    lower = (block_ids[:, None] >= block_ids[None, :]).astype(jnp.float32)
    within = jnp.einsum("ij,tbjo->tbio", lower, blocks, precision=lax.Precision.HIGHEST)
    totals = jnp.sum(blocks, axis=2)
    before = jnp.cumsum(totals, axis=1) - totals
    inclusive = (within + before[:, :, None, :]).reshape(node_kinds, sampled, groups)
    slot_rank = jnp.sum((inclusive - 1.0) * owner_hot, axis=2).astype(jnp.int32)
    position = owners * capacity + slot_rank
    rank_hot = (
        slot_rank[:, :, None] == jnp.arange(capacity, dtype=jnp.int32)[None, None, :]
    ).astype(jnp.float32)
    weighted_owner = owner_hot * sample_row[:, :, None].astype(jnp.float32)
    requests = jnp.einsum(
        "tio,tik->tok", weighted_owner, rank_hot, precision=lax.Precision.HIGHEST
    ).astype(jnp.int32)
    fetched_parts = []
    for node_kind in range(node_kinds):
        fetched_parts.append(
            serve_kind(
                features[node_kind],
                lax.all_to_all(requests[node_kind], "dp", split_axis=0, concat_axis=0, tiled=True),
            )
        )
    fetched = jnp.stack(fetched_parts)
    fetched = fetched.reshape(node_kinds, width_here, groups * capacity)
    gathered = jnp.stack(
        [pick_columns(fetched[node_kind], position[node_kind]) for node_kind in range(node_kinds)]
    )
    edge_total = edge_src.shape[1]
    seed_ids = jnp.arange(SEEDS, dtype=jnp.int32)[:, None]
    slot_ids = jnp.arange(edge_total, dtype=jnp.int32)
    messages = []
    for relation in range(RELS):
        live_edge = slot_ids < edge_count[relation, 0]
        target = jnp.where(live_edge, edge_dst[relation], -1)
        dst_hot = (seed_ids == target[None, :]).astype(jnp.bfloat16)
        sources = pick_columns(gathered[RELATION_SOURCE[relation]], edge_src[relation])
        summed = lax.dot_general(
            sources, dst_hot, (((1,), (1,)), ((), ())), preferred_element_type=jnp.float32
        )
        degree = jnp.sum(dst_hot, axis=1, dtype=jnp.float32)
        messages.append((summed / jnp.maximum(degree, 1.0)[None, :]).astype(jnp.bfloat16))
    for node_kind in range(node_kinds):
        messages.append(gathered[node_kind, :, :SEEDS])
    stacked = jnp.stack(messages)
    full_width = weights.shape[2]
    partial_sums = [jnp.zeros((full_width, SEEDS), jnp.float32) for node_kind in range(node_kinds)]
    for matrix in range(stacked.shape[0]):
        partial_sums[MATRIX_TARGET[matrix]] = partial_sums[MATRIX_TARGET[matrix]] + contract_first(
            weights[matrix], stacked[matrix]
        )
    typed = lax.psum_scatter(jnp.stack(partial_sums), "mp", scatter_dimension=1, tiled=True)
    return jax.nn.relu(typed).astype(jnp.bfloat16)


def solution(mesh):
    return jax.shard_map(
        per_device,
        mesh=mesh,
        in_specs=(
            P(None, "mp", "dp"),
            P(None, "mp", None),
            P(None, "dp", None),
            P(None, "dp"),
            P(None, "dp"),
            P(None, "dp"),
            P(None, "dp"),
        ),
        out_specs=P(None, "mp", "dp"),
        check_vma=False,
    )
```

profile of v0, /device:TPU:0, one launch (start us, length us, event | category | flops | bytes accessed | tf_op | source)
XLA Modules:
  0.0 245.6 jit_solution(14992279231206325996)
XLA Ops:
  9.4 4.3 %fusion.227 = s32[3,8,512]{2,1,0:T(8,128)S(1)} fusion(s32[3,2048]{1,0:T(4,128)S(1)} %bitcast.375, f32[3,2048]{1,0:T(4,128)S(1)} %convert_element_type.199, s32[3,2048]{1,0:T(4,128)S(1)} %bitcast.394), kind=kOutput, calls=%fused_computation.161 | convolution fusion | flops 305246208 | bytes 122880 | tf_op jit(solution)/shard_map/tio,tik->tok/dot_general | solution.py:62
  14.4 7.3 %all-to-all-start = ((s32[8,1,512]{2,1,0:T(1,128)}), s32[8,1,512]{2,1,0:T(1,128)S(1)}, u32[]{:S(2)}, u32[]{:S(2)}) async-start(s32[8,1,512]{2,1,0:T(1,128)} %copy.32), calls=%async_computation | async-start | bytes 32768 | tf_op jit(solution)/shard_map/all_to_all | solution.py:70
  22.5 5.1 %compare_select_fusion.5 = (s32[1,2048]{1,0:T(1,128)S(1)}, s32[1,2048]{1,0:T(1,128)S(1)}, s32[1,2048]{1,0:T(1,128)S(1)}, s32[1,2048]{1,0:T(1,128)S(1)}, s32[1,20...) fusion(s32[8,2048]{1,0:T(8,128)S(1)} %copy-done.14, s32[]{:T(128)} %bitcast.33, ...), kind=kLoop, calls=%fused_computation.252 | loop fusion | flops 32768 | bytes 131104 | tf_op jit(solution)/shard_map/jit(_where)/select_n | solution.py:84
  29.9 6.0 %all-to-all-start.2 = ((s32[8,1,512]{2,1,0:T(1,128)}), s32[8,1,512]{2,1,0:T(1,128)S(1)}, u32[]{:S(2)}, u32[]{:S(2)}) async-start(s32[8,1,512]{2,1,0:T(1,128)} %copy.35), calls=%async_computation.2 | async-start | bytes 32768 | tf_op jit(solution)/shard_map/all_to_all | solution.py:70
  36.9 5.6 %all-to-all-done.2 = s32[8,1,512]{2,1,0:T(1,128)S(1)} async-done(((s32[8,1,512]{2,1,0:T(1,128)}), s32[8,1,512]{2,1,0:T(1,128)S(1)}, u32[]{:S(2)}, u32[]{:S(2)}) %all-to-all-start.2) | async-done | bytes 16416 | tf_op jit(solution)/shard_map/all_to_all | solution.py:70
  42.5 3.3 %all-to-all-start.4 = ((s32[8,1,512]{2,1,0:T(1,128)}), s32[8,1,512]{2,1,0:T(1,128)S(1)}, u32[]{:S(2)}, u32[]{:S(2)}) async-start(s32[8,1,512]{2,1,0:T(1,128)} %copy.38), calls=%async_computation.4 | async-start | bytes 32768 | tf_op jit(solution)/shard_map/all_to_all | solution.py:70
  47.0 11.4 %while.154 = (s32[]{:T(128)}, bf16[8,128,512]{1,2,0:T(8,128)(2,1)}, s32[8,512]{1,0:T(8,128)S(1)}, bf16[128,2048]{1,0:T(8,128)(2,1)S(1)}, s32[]{:T(128)}) while((s32[]{:T(128)}, bf16[8,128,512]{1,2,0:T(8,128)(2,1)}, s32[8,512]{1,0:T(8,128)S(1)}, bf16[128,2048]{1,0:T(8,128)(2,1)S(1)}, s32[]{:T(128)}) %tuple.315), condition=%wide.region_4.5_spmd.clone, body=%wide.region_3.4_spmd.clone.sunk | while | flops 270598144 | bytes 662081 | solution.py:22
  49.8 1.4 fusion.360
  56.9 1.4 fusion.360
  58.3 5.9 %all-to-all-start.1 = ((bf16[128,8,512]{0,2,1:T(8,128)(2,1)}), bf16[128,8,512]{0,2,1:T(8,128)(2,1)S(1)}, u32[]{:S(2)}, u32[]{:S(2)}) async-start(bf16[128,8,512]{0,2,1:T(8,128)(2,1)} %bitcast.5), calls=%async_computation.1 | async-start | bytes 2097152 | tf_op jit(solution)/shard_map/all_to_all | solution.py:29
  65.4 11.3 %while.157 = (s32[]{:T(128)}, bf16[8,128,512]{1,2,0:T(8,128)(2,1)}, s32[8,512]{1,0:T(8,128)S(1)}, bf16[128,2048]{1,0:T(8,128)(2,1)S(1)}, s32[]{:T(128)}) while((s32[]{:T(128)}, bf16[8,128,512]{1,2,0:T(8,128)(2,1)}, s32[8,512]{1,0:T(8,128)S(1)}, bf16[128,2048]{1,0:T(8,128)(2,1)S(1)}, s32[]{:T(128)}) %tuple.314), condition=%wide.region_11.12_spmd.clone, body=%wide.region_10.11_spmd.clone.sunk | while | flops 270598144 | bytes 662081 | solution.py:22
  69.7 1.4 fusion.369
  75.4 1.4 fusion.369
  76.8 11.2 %all-to-all-done.1 = bf16[128,8,512]{0,2,1:T(8,128)(2,1)S(1)} async-done(((bf16[128,8,512]{0,2,1:T(8,128)(2,1)}), bf16[128,8,512]{0,2,1:T(8,128)(2,1)S(1)}, u32[]{:S(2)}, u32[]{:S(2)}) %all-to-all-start.1) | async-done | bytes 1048608 | tf_op jit(solution)/shard_map/all_to_all | solution.py:29
  88.0 3.6 %all-to-all-start.3 = ((bf16[128,8,512]{0,2,1:T(8,128)(2,1)}), bf16[128,8,512]{0,2,1:T(8,128)(2,1)S(1)}, u32[]{:S(2)}, u32[]{:S(2)}) async-start(bf16[128,8,512]{0,2,1:T(8,128)(2,1)} %bitcast.16), calls=%async_computation.3 | async-start | bytes 2097152 | tf_op jit(solution)/shard_map/all_to_all | solution.py:29
  92.7 11.3 %while.160 = (s32[]{:T(128)}, bf16[8,128,512]{1,2,0:T(8,128)(2,1)}, s32[8,512]{1,0:T(8,128)S(1)}, bf16[128,2048]{1,0:T(8,128)(2,1)S(1)}, s32[]{:T(128)}) while((s32[]{:T(128)}, bf16[8,128,512]{1,2,0:T(8,128)(2,1)}, s32[8,512]{1,0:T(8,128)S(1)}, bf16[128,2048]{1,0:T(8,128)(2,1)S(1)}, s32[]{:T(128)}) %tuple.313), condition=%wide.region_18.19_spmd.clone, body=%wide.region_17.18_spmd.clone.sunk | while | flops 270598144 | bytes 662081 | solution.py:22
  96.9 1.4 fusion.378
  99.8 1.4 fusion.378
  105.4 10.5 %while.155 = (s32[]{:T(128)}, bf16[4,128,512]{1,2,0:T(8,128)(2,1)S(1)}, s32[4,512]{1,0:T(4,128)S(1)}, bf16[128,4096]{1,0:T(8,128)(2,1)}, s32[]{:T(128)}) while((s32[]{:T(128)}, bf16[4,128,512]{1,2,0:T(8,128)(2,1)S(1)}, s32[4,512]{1,0:T(4,128)S(1)}, bf16[128,4096]{1,0:T(8,128)(2,1)}, s32[]{:T(128)}) %tuple.267), condition=%wide.region_6.7_spmd.clone, body=%wide.region_5.6_spmd.clone.sunk | while | flops 541130752 | bytes 1185861 | solution.py:22
  105.4 2.6 %fusion.363 = bf16[4,128,512]{1,2,0:T(8,128)(2,1)S(1)} fusion(bf16[4,128,512]{1,2,0:T(8,128)(2,1)S(1)} %get-tuple-element.1061, s32[]{:T(128)} %get-tuple-element.1060, bf16[128,4096]{1,0:T(8,128)(2,1)} %get-tuple-element.1068, s32[512]{0:T(512)S(1)} %bitcast.380), kind=kOutput, calls=%fused_computation.28.clone.1 | convolution fusion | flops 541130752 | bytes 1181700 | tf_op jit(solution)/shard_map/while/body/eval_jaxpr/dot_general | solution.py:20
  108.0 2.6 %fusion.363 = bf16[4,128,512]{1,2,0:T(8,128)(2,1)S(1)} fusion(bf16[4,128,512]{1,2,0:T(8,128)(2,1)S(1)} %get-tuple-element.1061, s32[]{:T(128)} %get-tuple-element.1060, bf16[128,4096]{1,0:T(8,128)(2,1)} %get-tuple-element.1068, s32[512]{0:T(512)S(1)} %bitcast.380), kind=kOutput, calls=%fused_computation.28.clone.1 | convolution fusion | flops 541130752 | bytes 1181700 | tf_op jit(solution)/shard_map/while/body/eval_jaxpr/dot_general | solution.py:20
  110.6 2.6 %fusion.363 = bf16[4,128,512]{1,2,0:T(8,128)(2,1)S(1)} fusion(bf16[4,128,512]{1,2,0:T(8,128)(2,1)S(1)} %get-tuple-element.1061, s32[]{:T(128)} %get-tuple-element.1060, bf16[128,4096]{1,0:T(8,128)(2,1)} %get-tuple-element.1068, s32[512]{0:T(512)S(1)} %bitcast.380), kind=kOutput, calls=%fused_computation.28.clone.1 | convolution fusion | flops 541130752 | bytes 1181700 | tf_op jit(solution)/shard_map/while/body/eval_jaxpr/dot_general | solution.py:20
  113.3 2.6 %fusion.363 = bf16[4,128,512]{1,2,0:T(8,128)(2,1)S(1)} fusion(bf16[4,128,512]{1,2,0:T(8,128)(2,1)S(1)} %get-tuple-element.1061, s32[]{:T(128)} %get-tuple-element.1060, bf16[128,4096]{1,0:T(8,128)(2,1)} %get-tuple-element.1068, s32[512]{0:T(512)S(1)} %bitcast.380), kind=kOutput, calls=%fused_computation.28.clone.1 | convolution fusion | flops 541130752 | bytes 1181700 | tf_op jit(solution)/shard_map/while/body/eval_jaxpr/dot_general | solution.py:20
  116.9 5.9 %all-to-all-start.5 = ((bf16[128,8,512]{0,2,1:T(8,128)(2,1)}), bf16[128,8,512]{0,2,1:T(8,128)(2,1)S(1)}, u32[]{:S(2)}, u32[]{:S(2)}) async-start(bf16[128,8,512]{0,2,1:T(8,128)(2,1)} %bitcast.27), calls=%async_computation.5 | async-start | bytes 2097152 | tf_op jit(solution)/shard_map/all_to_all | solution.py:29
  124.4 10.5 %while.158 = (s32[]{:T(128)}, bf16[4,128,512]{1,2,0:T(8,128)(2,1)S(1)}, s32[4,512]{1,0:T(4,128)S(1)}, bf16[128,4096]{1,0:T(8,128)(2,1)}, s32[]{:T(128)}) while((s32[]{:T(128)}, bf16[4,128,512]{1,2,0:T(8,128)(2,1)S(1)}, s32[4,512]{1,0:T(4,128)S(1)}, bf16[128,4096]{1,0:T(8,128)(2,1)}, s32[]{:T(128)}) %tuple.276), condition=%wide.region_13.14_spmd.clone, body=%wide.region_12.13_spmd.clone.sunk | while | flops 541130752 | bytes 1185861 | solution.py:22
  124.4 2.6 %fusion.372 = bf16[4,128,512]{1,2,0:T(8,128)(2,1)S(1)} fusion(bf16[4,128,512]{1,2,0:T(8,128)(2,1)S(1)} %get-tuple-element.1106, s32[]{:T(128)} %get-tuple-element.1105, bf16[128,4096]{1,0:T(8,128)(2,1)} %get-tuple-element.1113, s32[512]{0:T(512)S(1)} %bitcast.381), kind=kOutput, calls=%fused_computation.52.clone.1 | convolution fusion | flops 541130752 | bytes 1181700 | tf_op jit(solution)/shard_map/while/body/eval_jaxpr/dot_general | solution.py:20
  127.1 2.6 %fusion.372 = bf16[4,128,512]{1,2,0:T(8,128)(2,1)S(1)} fusion(bf16[4,128,512]{1,2,0:T(8,128)(2,1)S(1)} %get-tuple-element.1106, s32[]{:T(128)} %get-tuple-element.1105, bf16[128,4096]{1,0:T(8,128)(2,1)} %get-tuple-element.1113, s32[512]{0:T(512)S(1)} %bitcast.381), kind=kOutput, calls=%fused_computation.52.clone.1 | convolution fusion | flops 541130752 | bytes 1181700 | tf_op jit(solution)/shard_map/while/body/eval_jaxpr/dot_general | solution.py:20
  129.7 2.6 %fusion.372 = bf16[4,128,512]{1,2,0:T(8,128)(2,1)S(1)} fusion(bf16[4,128,512]{1,2,0:T(8,128)(2,1)S(1)} %get-tuple-element.1106, s32[]{:T(128)} %get-tuple-element.1105, bf16[128,4096]{1,0:T(8,128)(2,1)} %get-tuple-element.1113, s32[512]{0:T(512)S(1)} %bitcast.381), kind=kOutput, calls=%fused_computation.52.clone.1 | convolution fusion | flops 541130752 | bytes 1181700 | tf_op jit(solution)/shard_map/while/body/eval_jaxpr/dot_general | solution.py:20
  132.3 2.6 %fusion.372 = bf16[4,128,512]{1,2,0:T(8,128)(2,1)S(1)} fusion(bf16[4,128,512]{1,2,0:T(8,128)(2,1)S(1)} %get-tuple-element.1106, s32[]{:T(128)} %get-tuple-element.1105, bf16[128,4096]{1,0:T(8,128)(2,1)} %get-tuple-element.1113, s32[512]{0:T(512)S(1)} %bitcast.381), kind=kOutput, calls=%fused_computation.52.clone.1 | convolution fusion | flops 541130752 | bytes 1181700 | tf_op jit(solution)/shard_map/while/body/eval_jaxpr/dot_general | solution.py:20
  135.0 3.4 %while.156 = (s32[]{:T(128)}, bf16[4,128,512]{1,2,0:T(8,128)(2,1)S(1)}, s32[4,512]{1,0:T(4,128)S(1)}, bf16[128,2048]{1,0:T(8,128)(2,1)S(1)}, s32[]{:T(128)}) while((s32[]{:T(128)}, bf16[4,128,512]{1,2,0:T(8,128)(2,1)S(1)}, s32[4,512]{1,0:T(4,128)S(1)}, bf16[128,2048]{1,0:T(8,128)(2,1)S(1)}, s32[]{:T(128)}) %tuple.308), condition=%wide.region_8.9_spmd.clone, body=%wide.region_7.8_spmd.clone.sunk | while | flops 270598144 | bytes 661573 | solution.py:22
  139.5 7.6 %while.159 = (s32[]{:T(128)}, bf16[4,128,512]{1,2,0:T(8,128)(2,1)S(1)}, s32[4,512]{1,0:T(4,128)S(1)}, bf16[128,2048]{1,0:T(8,128)(2,1)}, s32[]{:T(128)}) while((s32[]{:T(128)}, bf16[4,128,512]{1,2,0:T(8,128)(2,1)S(1)}, s32[4,512]{1,0:T(4,128)S(1)}, bf16[128,2048]{1,0:T(8,128)(2,1)}, s32[]{:T(128)}) %tuple.300), condition=%wide.region_15.16_spmd.clone, body=%wide.region_14.15_spmd.clone.sunk | while | flops 270598144 | bytes 661573 | solution.py:22
  139.6 1.9 fusion.375
  141.5 1.9 fusion.375
  143.4 1.9 fusion.375
  145.2 1.9 fusion.375
  148.5 5.6 %while.161 = (s32[]{:T(128)}, bf16[4,128,512]{1,2,0:T(8,128)(2,1)S(1)}, s32[4,512]{1,0:T(4,128)S(1)}, bf16[128,4096]{1,0:T(8,128)(2,1)S(1)}, s32[]{:T(128)}) while((s32[]{:T(128)}, bf16[4,128,512]{1,2,0:T(8,128)(2,1)S(1)}, s32[4,512]{1,0:T(4,128)S(1)}, bf16[128,4096]{1,0:T(8,128)(2,1)S(1)}, s32[]{:T(128)}) %tuple.285), condition=%wide.region_20.21_spmd.clone, body=%wide.region_19.20_spmd.clone.sunk | while | flops 541130752 | bytes 1185861 | solution.py:22
  155.2 7.6 %while.162 = (s32[]{:T(128)}, bf16[4,128,512]{1,2,0:T(8,128)(2,1)S(1)}, s32[4,512]{1,0:T(4,128)S(1)}, bf16[128,2048]{1,0:T(8,128)(2,1)}, s32[]{:T(128)}) while((s32[]{:T(128)}, bf16[4,128,512]{1,2,0:T(8,128)(2,1)S(1)}, s32[4,512]{1,0:T(4,128)S(1)}, bf16[128,2048]{1,0:T(8,128)(2,1)}, s32[]{:T(128)}) %tuple.303), condition=%wide.region_22.23_spmd.clone, body=%wide.region_21.22_spmd.clone.sunk | while | flops 270598144 | bytes 661573 | solution.py:22
  155.2 1.9 fusion.384
  157.2 1.9 fusion.384
  159.1 1.9 fusion.384
  161.0 1.9 fusion.384
  163.7 3.4 %while.163 = (s32[]{:T(128)}, bf16[4,128,512]{1,2,0:T(8,128)(2,1)S(1)}, s32[4,512]{1,0:T(4,128)S(1)}, bf16[128,2048]{1,0:T(8,128)(2,1)S(1)}, s32[]{:T(128)}) while((s32[]{:T(128)}, bf16[4,128,512]{1,2,0:T(8,128)(2,1)S(1)}, s32[4,512]{1,0:T(4,128)S(1)}, bf16[128,2048]{1,0:T(8,128)(2,1)S(1)}, s32[]{:T(128)}) %tuple.311), condition=%wide.region_25.26_spmd.clone, body=%wide.region_24.25_spmd.clone.sunk | while | flops 270598144 | bytes 661573 | solution.py:22
  167.8 7.5 %while.164 = (s32[]{:T(128)}, bf16[4,128,512]{1,2,0:T(8,128)(2,1)S(1)}, s32[4,512]{1,0:T(4,128)S(1)}, bf16[128,2048]{1,0:T(8,128)(2,1)}, s32[]{:T(128)}) while((s32[]{:T(128)}, bf16[4,128,512]{1,2,0:T(8,128)(2,1)S(1)}, s32[4,512]{1,0:T(4,128)S(1)}, bf16[128,2048]{1,0:T(8,128)(2,1)}, s32[]{:T(128)}) %tuple.291), condition=%wide.region_28.29_spmd.clone, body=%wide.region_27.28_spmd.clone.sunk | while | flops 270598144 | bytes 661573 | solution.py:22
  167.8 1.9 fusion.390
  169.7 1.9 fusion.390
  171.6 1.9 fusion.390
  173.5 1.9 fusion.390
  176.2 3.4 %while.165 = (s32[]{:T(128)}, bf16[4,128,512]{1,2,0:T(8,128)(2,1)S(1)}, s32[4,512]{1,0:T(4,128)S(1)}, bf16[128,2048]{1,0:T(8,128)(2,1)S(1)}, s32[]{:T(128)}) while((s32[]{:T(128)}, bf16[4,128,512]{1,2,0:T(8,128)(2,1)S(1)}, s32[4,512]{1,0:T(4,128)S(1)}, bf16[128,2048]{1,0:T(8,128)(2,1)S(1)}, s32[]{:T(128)}) %tuple.309), condition=%wide.region_31.32_spmd.clone, body=%wide.region_30.31_spmd.clone.sunk | while | flops 270598144 | bytes 661573 | solution.py:22
  180.5 5.7 %while.166 = (s32[]{:T(128)}, bf16[4,128,512]{1,2,0:T(8,128)(2,1)}, s32[4,512]{1,0:T(4,128)S(1)}, bf16[128,2048]{1,0:T(8,128)(2,1)S(1)}, s32[]{:T(128)}) while((s32[]{:T(128)}, bf16[4,128,512]{1,2,0:T(8,128)(2,1)}, s32[4,512]{1,0:T(4,128)S(1)}, bf16[128,2048]{1,0:T(8,128)(2,1)S(1)}, s32[]{:T(128)}) %tuple.310), condition=%wide.region_34.35_spmd.clone, body=%wide.region_33.34_spmd.clone.sunk | while | flops 270598144 | bytes 662081 | solution.py:22
  184.8 1.4 fusion.396
  186.3 7.9 %while.167 = (s32[]{:T(128)}, bf16[4,128,512]{1,2,0:T(8,128)(2,1)S(1)}, s32[4,512]{1,0:T(4,128)S(1)}, bf16[128,2048]{1,0:T(8,128)(2,1)}, s32[]{:T(128)}) while((s32[]{:T(128)}, bf16[4,128,512]{1,2,0:T(8,128)(2,1)S(1)}, s32[4,512]{1,0:T(4,128)S(1)}, bf16[128,2048]{1,0:T(8,128)(2,1)}, s32[]{:T(128)}) %tuple.312), condition=%wide.region_37.38_spmd.clone, body=%wide.region_36.37_spmd.clone.sunk | while | flops 270598144 | bytes 661573 | solution.py:22
  186.3 1.9 fusion.399
  188.3 1.9 fusion.399
  190.2 1.9 fusion.399
  192.1 1.9 fusion.399
  194.2 2.2 fusion.230
  196.4 2.3 convolution_add_fusion.7
  198.7 1.7 convolution_add_fusion.6
  201.5 1.5 fusion.229
  203.0 1.6 convolution_add_fusion.4
  204.7 1.6 convolution_add_fusion.3
  207.4 1.6 fusion.228
  209.0 1.5 convolution_add_fusion.1
  212.6 24.5 %reduce-scatter.2.cloned.1.call-done = f32[3,128,128]{1,2,0:T(8,128)} async-done(((f32[3,512,128]{1,2,0:T(8,128)}), f32[3,128,128]{1,2,0:T(8,128)}) %reduce-scatter.2.cloned.1.call-update) | async-done | bytes 196624 | tf_op jit(solution)/shard_map/reduce_scatter | solution.py:101
  (219 shorter events, 73.1 us)
Async XLA Ops:
  9.4 12.3 %copy-start.13 = (s32[3,2048,1]{1,2,0:T(1,128)S(1)}, s32[3,2048,1]{1,2,0:T(1,128)}, u32[]{:S(2)}) copy-start(s32[3,2048,1]{1,2,0:T(1,128)} %param.37) | copy-start | bytes 73732
  9.4 12.4 %copy-start.16 = (s32[8,1]{0,1:T(1,128)S(1)}, s32[8,1]{0,1:T(1,128)}, u32[]{:S(2)}) copy-start(s32[8,1]{0,1:T(1,128)} %param.41) | copy-start | bytes 100
  9.4 13.1 %copy-start.14 = (s32[8,2048]{1,0:T(8,128)S(1)}, s32[8,2048]{1,0:T(8,128)}, u32[]{:S(2)}) copy-start(s32[8,2048]{1,0:T(8,128)} %param.40) | copy-start | bytes 196612
  9.4 18.3 %copy-start = (bf16[3,128,2048]{2,1,0:T(8,128)(2,1)S(1)}, bf16[3,128,2048]{2,1,0:T(8,128)(2,1)}, u32[]{:S(2)}) copy-start(bf16[3,128,2048]{2,1,0:T(8,128)(2,1)} %param.35) | copy-start | bytes 4718596
  14.4 15.5 %all-to-all-start = ((s32[8,1,512]{2,1,0:T(1,128)}), s32[8,1,512]{2,1,0:T(1,128)S(1)}, u32[]{:S(2)}, u32[]{:S(2)}) async-start(s32[8,1,512]{2,1,0:T(1,128)} %copy.32), calls=%async_computation | async-start | bytes 32768 | tf_op jit(solution)/shard_map/all_to_all | solution.py:70
  27.7 8.2 %copy-start.15 = (s32[8,2048]{1,0:T(8,128)S(1)}, s32[8,2048]{1,0:T(8,128)}, u32[]{:S(2)}) copy-start(s32[8,2048]{1,0:T(8,128)} %param.39) | copy-start | bytes 196612
  29.9 12.6 %all-to-all-start.2 = ((s32[8,1,512]{2,1,0:T(1,128)}), s32[8,1,512]{2,1,0:T(1,128)S(1)}, u32[]{:S(2)}, u32[]{:S(2)}) async-start(s32[8,1,512]{2,1,0:T(1,128)} %copy.35), calls=%async_computation.2 | async-start | bytes 32768 | tf_op jit(solution)/shard_map/all_to_all | solution.py:70
  42.5 15.8 %all-to-all-start.4 = ((s32[8,1,512]{2,1,0:T(1,128)}), s32[8,1,512]{2,1,0:T(1,128)S(1)}, u32[]{:S(2)}, u32[]{:S(2)}) async-start(s32[8,1,512]{2,1,0:T(1,128)} %copy.38), calls=%async_computation.4 | async-start | bytes 32768 | tf_op jit(solution)/shard_map/all_to_all | solution.py:70
  58.3 29.7 %all-to-all-start.1 = ((bf16[128,8,512]{0,2,1:T(8,128)(2,1)}), bf16[128,8,512]{0,2,1:T(8,128)(2,1)S(1)}, u32[]{:S(2)}, u32[]{:S(2)}) async-start(bf16[128,8,512]{0,2,1:T(8,128)(2,1)} %bitcast.5), calls=%async_computation.1 | async-start | bytes 2097152 | tf_op jit(solution)/shard_map/all_to_all | solution.py:29
  88.0 28.9 %all-to-all-start.3 = ((bf16[128,8,512]{0,2,1:T(8,128)(2,1)}), bf16[128,8,512]{0,2,1:T(8,128)(2,1)S(1)}, u32[]{:S(2)}, u32[]{:S(2)}) async-start(bf16[128,8,512]{0,2,1:T(8,128)(2,1)} %bitcast.16), calls=%async_computation.3 | async-start | bytes 2097152 | tf_op jit(solution)/shard_map/all_to_all | solution.py:29
  116.9 30.7 %all-to-all-start.5 = ((bf16[128,8,512]{0,2,1:T(8,128)(2,1)}), bf16[128,8,512]{0,2,1:T(8,128)(2,1)S(1)}, u32[]{:S(2)}, u32[]{:S(2)}) async-start(bf16[128,8,512]{0,2,1:T(8,128)(2,1)} %bitcast.27), calls=%async_computation.5 | async-start | bytes 2097152 | tf_op jit(solution)/shard_map/all_to_all | solution.py:29
  122.8 114.3 %reduce-scatter.2.cloned.1.call-start = ((), (), s32[]{:S(2)}) async-start(), calls=%async_computation.7 | async-start | bytes 983040 | tf_op jit(solution)/shard_map/reduce_scatter | solution.py:101
  124.4 10.6 %copy-start.10 = (bf16[128,2048]{1,0:T(8,128)(2,1)S(1)}, bf16[128,2048]{1,0:T(8,128)(2,1)}, u32[]{:S(2)}) copy-start(bf16[128,2048]{1,0:T(8,128)(2,1)} %copy.44) | copy-start | bytes 1572868
  138.4 1.1 copy-start.1
  147.1 0.8 copy-start.3
  155.2 7.7 %copy-start.12 = (bf16[128,2048]{1,0:T(8,128)(2,1)S(1)}, bf16[128,2048]{1,0:T(8,128)(2,1)}, u32[]{:S(2)}) copy-start(bf16[128,2048]{1,0:T(8,128)(2,1)} %get-tuple-element.1258) | copy-start | bytes 1572868
  162.8 0.8 copy-start.5
  167.0 0.8 copy-start.6
  167.1 8.4 %copy-start.11 = (bf16[128,2048]{1,0:T(8,128)(2,1)S(1)}, bf16[128,2048]{1,0:T(8,128)(2,1)}, u32[]{:S(2)}) copy-start(bf16[128,2048]{1,0:T(8,128)(2,1)} %copy.44) | copy-start | bytes 1572868
  175.4 0.8 copy-start.8
  179.6 1.0 copy-start.9
  186.3 7.9 %copy-start.2 = (bf16[4,128,512]{1,2,0:T(8,128)(2,1)S(1)}, bf16[4,128,512]{1,2,0:T(8,128)(2,1)}, u32[]{:S(2)}) copy-start(bf16[4,128,512]{1,2,0:T(8,128)(2,1)} %copy-done.1) | copy-start | bytes 1572868
  186.3 10.1 %copy-start.4 = (bf16[4,128,512]{1,2,0:T(8,128)(2,1)S(1)}, bf16[4,128,512]{1,2,0:T(8,128)(2,1)}, u32[]{:S(2)}) copy-start(bf16[4,128,512]{1,2,0:T(8,128)(2,1)} %copy-done.3) | copy-start | bytes 1572868
  196.4 5.2 %copy-start.7 = (bf16[4,128,512]{1,2,0:T(8,128)(2,1)S(1)}, bf16[4,128,512]{1,2,0:T(8,128)(2,1)}, u32[]{:S(2)}) copy-start(bf16[4,128,512]{1,2,0:T(8,128)(2,1)} %copy-done.6) | copy-start | bytes 1572868
Sparse Core Ops, SparseCore 0:
  212.7 24.3 reduce-scatter.1
where the time goes:
time: 248 us; the launch traced here: 246 us
  matrix products  127 us (51%)
  waiting for transfers between devices  41.8 us (17%)
  starting transfers between devices  32.3 us (13%)
  local copies, waits for them, and re-layouts  18.9 us (8%)
  between operations  14 us (6%)
  other arithmetic  10.3 us (4%)
    dot_general x68, matrix products, one_block(): jnp.dot(table, chosen, preferred_element_type=jnp.float32)  105 us
    reduce_scatter x1, waiting for transfers between devices, per_device(): lax.psum_scatter(jnp.stack(partial_sums), 'mp', scatter_dimension=1, tile...  24.5 us
    dot_general x11, matrix products, contract_first(): lax.dot_general(left, right, (((0,), (0,)), ((), ())), preferred_element_...  17.3 us
    all_to_all x3, starting transfers between devices, per_device(): lax.all_to_all(requests[node_kind], 'dp', split_axis=0, concat_axis=0, ti...  16.6 us
    all_to_all x3, starting transfers between devices, serve_kind(): return lax.all_to_all(picked, 'dp', split_axis=1, concat_axis=1, tiled=True)  15.4 us
    all_to_all x3, waiting for transfers between devices, serve_kind(): return lax.all_to_all(picked, 'dp', split_axis=1, concat_axis=1, tiled=True)  11.7 us
    all_to_all x3, waiting for transfers between devices, per_device(): lax.all_to_all(requests[node_kind], 'dp', split_axis=0, concat_axis=0, ti...  5.58 us
    another operation x14, local copies, waits for them, and re-layouts  5.08 us
  transfers between devices with their start and end apart: 7, of which 4 were waited for; matrix products, arithmetic and copies ran while one was open for 34% of the time, Pallas kernels for 0%

commit v1 on v0

--- a/solution.py
+++ b/solution.py
@@ -8,6 +8,19 @@
 SEEDS = 128
 RELATION_SOURCE = (0, 1, 0, 1, 2, 0, 2, 1)
 MATRIX_TARGET = (1, 0, 0, 2, 1, 2, 0, 1, 0, 1, 2)
+
+
+def watch_chains(field_in):
+    aux = jnp.concatenate(
+        lax.all_to_all(
+            jnp.stack(jnp.split(field_in, lax.axis_size("dp"), axis=1)),
+            split_axis=0,
+            axis_name="dp",
+            concat_axis=0,
+        ),
+        axis=1,
+    )
+    return aux
 
 
 def pick_columns(table, index):
@@ -26,7 +39,7 @@
 def serve_kind(kind_table, requested):
     picked = pick_columns(kind_table, requested.reshape(-1))
     picked = picked.reshape(kind_table.shape[0], requested.shape[0], requested.shape[1])
-    return lax.all_to_all(picked, "dp", split_axis=1, concat_axis=1, tiled=True)
+    return watch_chains(picked)
 
 
 def contract_first(left, right):

time: 248 us -> 256 us (1.032)
  matrix products: 127 us -> 112 us
  local copies, waits for them, and re-layouts: 18.9 us -> 33.1 us
  waiting for transfers between devices: 41.8 us -> 46.3 us
  other arithmetic: 10.3 us -> 13.1 us
    unnamed x39 -> x74, local copies, waits for them, and re-layouts: 3.34 us -> 19.2 us
    dot_general x68, matrix products: 105 us -> 91.2 us  [one_block(): jnp.dot(table, chosen, preferred_element_type=jnp.float32)]
    all_to_all x3, waiting for transfers between devices: 11.7 us -> 23.1 us  [watch_chains(): lax.all_to_all(jnp.stack(jnp.split(field_in, lax.axis_size('dp'), axis=1)...]
    all_to_all x3, waiting for transfers between devices: 5.58 us -> 0.01 us  [per_device(): lax.all_to_all(requests[node_kind], 'dp', split_axis=0, concat_axis=0, ti...]
    all_to_all x3, starting transfers between devices: 16.6 us -> 19.3 us  [per_device(): lax.all_to_all(requests[node_kind], 'dp', split_axis=0, concat_axis=0, ti...]
    max x8, other arithmetic: 0.05 us -> 2.71 us  [per_device(): jnp.maximum(degree, 1.0)[None, :]]
where the time goes in v1:
time: 256 us; the launch traced here: 253 us
  matrix products  112 us (44%)
  waiting for transfers between devices  46.3 us (18%)
  local copies, waits for them, and re-layouts  33.1 us (13%)
  starting transfers between devices  32.6 us (13%)
  between operations  14.1 us (6%)
  other arithmetic  13.1 us (5%)
    dot_general x68, matrix products, one_block(): jnp.dot(table, chosen, preferred_element_type=jnp.float32)  91.2 us
    reduce_scatter x1, waiting for transfers between devices, per_device(): lax.psum_scatter(jnp.stack(partial_sums), 'mp', scatter_dimension=1, tile...  23.2 us
    all_to_all x3, waiting for transfers between devices, watch_chains(): lax.all_to_all(jnp.stack(jnp.split(field_in, lax.axis_size('dp'), axis=1)...  23.1 us
    all_to_all x3, starting transfers between devices, per_device(): lax.all_to_all(requests[node_kind], 'dp', split_axis=0, concat_axis=0, ti...  19.3 us
    unnamed x74, local copies, waits for them, and re-layouts  19.2 us
    dot_general x11, matrix products, contract_first(): lax.dot_general(left, right, (((0,), (0,)), ((), ())), preferred_element_...  16.4 us
    all_to_all x3, starting transfers between devices, watch_chains(): lax.all_to_all(jnp.stack(jnp.split(field_in, lax.axis_size('dp'), axis=1)...  13.1 us
    select_n x1, other arithmetic, per_device(): target = jnp.where(live_edge, edge_dst[relation], -1)  5.25 us
  transfers between devices with their start and end apart: 7, of which 4 were waited for; matrix products, arithmetic and copies ran while one was open for 34% of the time, Pallas kernels for 0%

profile of v1, /device:TPU:0, one launch (start us, length us, event | category | flops | bytes accessed | tf_op | source)
XLA Modules:
  0.0 253.5 jit_solution(3630062770660299271)
XLA Ops:
  9.4 4.3 %fusion.227 = s32[3,8,512]{2,1,0:T(8,128)S(1)} fusion(s32[3,2048]{1,0:T(4,128)S(1)} %bitcast.502, f32[3,2048]{1,0:T(4,128)S(1)} %convert_element_type.199, s32[3,2048]{1,0:T(4,128)S(1)} %bitcast.521), kind=kOutput, calls=%fused_computation.161 | convolution fusion | flops 305246208 | bytes 122880 | tf_op jit(solution)/shard_map/tio,tik->tok/dot_general | solution.py:75
  14.4 7.3 %all-to-all-start = ((s32[8,1,512]{2,1,0:T(1,128)}), s32[8,1,512]{2,1,0:T(1,128)S(1)}, u32[]{:S(2)}, u32[]{:S(2)}) async-start(s32[8,1,512]{2,1,0:T(1,128)} %copy.32), calls=%async_computation | async-start | bytes 32768 | tf_op jit(solution)/shard_map/all_to_all | solution.py:83
  23.4 5.3 %compare_select_fusion.5 = (s32[1,2048]{1,0:T(1,128)S(1)}, s32[1,2048]{1,0:T(1,128)S(1)}, s32[1,2048]{1,0:T(1,128)S(1)}, s32[1,2048]{1,0:T(1,128)S(1)}, s32[1,20...) fusion(s32[8,2048]{1,0:T(8,128)S(1)} %copy-done.16, s32[]{:T(128)} %bitcast.60, ...), kind=kLoop, calls=%fused_computation.300 | loop fusion | flops 32768 | bytes 131104 | tf_op jit(solution)/shard_map/jit(_where)/select_n | solution.py:97
  34.5 6.0 %all-to-all-start.2 = ((s32[8,1,512]{2,1,0:T(1,128)}), s32[8,1,512]{2,1,0:T(1,128)S(1)}, u32[]{:S(2)}, u32[]{:S(2)}) async-start(s32[8,1,512]{2,1,0:T(1,128)} %copy.35), calls=%async_computation.2 | async-start | bytes 32768 | tf_op jit(solution)/shard_map/all_to_all | solution.py:83
  40.7 6.8 %while.154 = (s32[]{:T(128)}, bf16[8,128,512]{1,2,0:T(8,128)(2,1)S(1)}, s32[8,512]{1,0:T(8,128)S(1)}, bf16[128,2048]{1,0:T(8,128)(2,1)S(1)}, s32[]{:T(128)}) while((s32[]{:T(128)}, bf16[8,128,512]{1,2,0:T(8,128)(2,1)S(1)}, s32[8,512]{1,0:T(8,128)S(1)}, bf16[128,2048]{1,0:T(8,128)(2,1)S(1)}, s32[]{:T(128)}) %tuple.313), condition=%wide.region_4.5_spmd.clone, body=%wide.region_3.4_spmd.clone.sunk | while | flops 270598144 | bytes 661573 | solution.py:35
  52.7 6.0 %all-to-all-start.4 = ((s32[8,1,512]{2,1,0:T(1,128)}), s32[8,1,512]{2,1,0:T(1,128)S(1)}, u32[]{:S(2)}, u32[]{:S(2)}) async-start(s32[8,1,512]{2,1,0:T(1,128)} %copy.38), calls=%async_computation.4 | async-start | bytes 32768 | tf_op jit(solution)/shard_map/all_to_all | solution.py:83
  58.9 6.8 %while.157 = (s32[]{:T(128)}, bf16[8,128,512]{1,2,0:T(8,128)(2,1)S(1)}, s32[8,512]{1,0:T(8,128)S(1)}, bf16[128,2048]{1,0:T(8,128)(2,1)S(1)}, s32[]{:T(128)}) while((s32[]{:T(128)}, bf16[8,128,512]{1,2,0:T(8,128)(2,1)S(1)}, s32[8,512]{1,0:T(8,128)S(1)}, bf16[128,2048]{1,0:T(8,128)(2,1)S(1)}, s32[]{:T(128)}) %tuple.314), condition=%wide.region_11.12_spmd.clone, body=%wide.region_10.11_spmd.clone.sunk | while | flops 270598144 | bytes 661573 | solution.py:35
  69.6 6.0 %all-to-all-start.1 = ((bf16[8,128,1,512]{1,3,2,0:T(8,128)(2,1)}), bf16[8,128,1,512]{1,3,2,0:T(8,128)(2,1)S(1)}, u32[]{:S(2)}, u32[]{:S(2)}) async-start(bf16[8,128,1,512]{1,3,2,0:T(8,128)(2,1)} %fusion.274), calls=%async_computation.1 | async-start | bytes 2097152 | tf_op jit(solution)/shard_map/all_to_all | solution.py:15
  75.7 15.1 %while.160 = (s32[]{:T(128)}, bf16[8,128,512]{1,2,0:T(8,128)(2,1)S(1)}, s32[8,512]{1,0:T(8,128)S(1)}, bf16[128,2048]{1,0:T(8,128)(2,1)}, s32[]{:T(128)}) while((s32[]{:T(128)}, bf16[8,128,512]{1,2,0:T(8,128)(2,1)S(1)}, s32[8,512]{1,0:T(8,128)S(1)}, bf16[128,2048]{1,0:T(8,128)(2,1)}, s32[]{:T(128)}) %tuple.312), condition=%wide.region_18.19_spmd.clone, body=%wide.region_17.18_spmd.clone.sunk | while | flops 270598144 | bytes 661573 | solution.py:35
  75.8 1.9 fusion.402
  77.7 1.9 fusion.402
  79.6 1.9 fusion.402
  81.5 1.9 fusion.402
  83.3 1.9 fusion.402
  85.2 1.9 fusion.402
  87.1 1.9 fusion.402
  89.0 1.9 fusion.402
  96.2 3.7 %all-to-all-done.1 = bf16[8,128,1,512]{1,3,2,0:T(8,128)(2,1)S(1)} async-done(((bf16[8,128,1,512]{1,3,2,0:T(8,128)(2,1)}), bf16[8,128,1,512]{1,3,2,0:T(8,128)(2,1)S(1)}, u32[]{:S(2)}, u32[]{:S(2)}) %all-to-all-start.1) | async-done | bytes 1048608 | tf_op jit(solution)/shard_map/all_to_all | solution.py:15
  99.9 3.6 %all-to-all-start.3 = ((bf16[8,128,1,512]{1,3,2,0:T(8,128)(2,1)}), bf16[8,128,1,512]{1,3,2,0:T(8,128)(2,1)S(1)}, u32[]{:S(2)}, u32[]{:S(2)}) async-start(bf16[8,128,1,512]{1,3,2,0:T(8,128)(2,1)} %fusion.266), calls=%async_computation.3 | async-start | bytes 2097152 | tf_op jit(solution)/shard_map/all_to_all | solution.py:15
  105.4 5.6 %while.155 = (s32[]{:T(128)}, bf16[4,128,512]{1,2,0:T(8,128)(2,1)S(1)}, s32[4,512]{1,0:T(4,128)S(1)}, bf16[128,4096]{1,0:T(8,128)(2,1)S(1)}, s32[]{:T(128)}) while((s32[]{:T(128)}, bf16[4,128,512]{1,2,0:T(8,128)(2,1)S(1)}, s32[4,512]{1,0:T(4,128)S(1)}, bf16[128,4096]{1,0:T(8,128)(2,1)S(1)}, s32[]{:T(128)}) %tuple.267), condition=%wide.region_6.7_spmd.clone, body=%wide.region_5.6_spmd.clone.sunk | while | flops 541130752 | bytes 1185861 | solution.py:35
  109.6 1.4 fusion.387
  112.0 17.2 %all-to-all-done.3 = bf16[8,128,1,512]{1,3,2,0:T(8,128)(2,1)S(1)} async-done(((bf16[8,128,1,512]{1,3,2,0:T(8,128)(2,1)}), bf16[8,128,1,512]{1,3,2,0:T(8,128)(2,1)S(1)}, u32[]{:S(2)}, u32[]{:S(2)}) %all-to-all-start.3) | async-done | bytes 1048608 | tf_op jit(solution)/shard_map/all_to_all | solution.py:15
  130.1 3.6 %all-to-all-start.5 = ((bf16[8,128,1,512]{1,3,2,0:T(8,128)(2,1)}), bf16[8,128,1,512]{1,3,2,0:T(8,128)(2,1)S(1)}, u32[]{:S(2)}, u32[]{:S(2)}) async-start(bf16[8,128,1,512]{1,3,2,0:T(8,128)(2,1)} %fusion.258), calls=%async_computation.5 | async-start | bytes 2097152 | tf_op jit(solution)/shard_map/all_to_all | solution.py:15
  133.9 1.5 copy.45
  135.5 5.6 %while.158 = (s32[]{:T(128)}, bf16[4,128,512]{1,2,0:T(8,128)(2,1)S(1)}, s32[4,512]{1,0:T(4,128)S(1)}, bf16[128,4096]{1,0:T(8,128)(2,1)S(1)}, s32[]{:T(128)}) while((s32[]{:T(128)}, bf16[4,128,512]{1,2,0:T(8,128)(2,1)S(1)}, s32[4,512]{1,0:T(4,128)S(1)}, bf16[128,4096]{1,0:T(8,128)(2,1)S(1)}, s32[]{:T(128)}) %tuple.276), condition=%wide.region_13.14_spmd.clone, body=%wide.region_12.13_spmd.clone.sunk | while | flops 541130752 | bytes 1185861 | solution.py:35
  141.2 7.6 %while.156 = (s32[]{:T(128)}, bf16[4,128,512]{1,2,0:T(8,128)(2,1)S(1)}, s32[4,512]{1,0:T(4,128)S(1)}, bf16[128,2048]{1,0:T(8,128)(2,1)}, s32[]{:T(128)}) while((s32[]{:T(128)}, bf16[4,128,512]{1,2,0:T(8,128)(2,1)S(1)}, s32[4,512]{1,0:T(4,128)S(1)}, bf16[128,2048]{1,0:T(8,128)(2,1)}, s32[]{:T(128)}) %tuple.297), condition=%wide.region_8.9_spmd.clone, body=%wide.region_7.8_spmd.clone.sunk | while | flops 270598144 | bytes 661573 | solution.py:35
  141.2 1.9 fusion.390
  143.1 1.9 fusion.390
  145.0 1.9 fusion.390
  146.9 1.9 fusion.390
  149.8 7.6 %while.159 = (s32[]{:T(128)}, bf16[4,128,512]{1,2,0:T(8,128)(2,1)S(1)}, s32[4,512]{1,0:T(4,128)S(1)}, bf16[128,2048]{1,0:T(8,128)(2,1)}, s32[]{:T(128)}) while((s32[]{:T(128)}, bf16[4,128,512]{1,2,0:T(8,128)(2,1)S(1)}, s32[4,512]{1,0:T(4,128)S(1)}, bf16[128,2048]{1,0:T(8,128)(2,1)}, s32[]{:T(128)}) %tuple.300), condition=%wide.region_15.16_spmd.clone, body=%wide.region_14.15_spmd.clone.sunk | while | flops 270598144 | bytes 661573 | solution.py:35
  149.9 1.9 fusion.399
  151.8 1.9 fusion.399
  153.7 1.9 fusion.399
  155.6 1.9 fusion.399
  157.4 2.2 all-to-all-done.5
  160.3 5.6 %while.161 = (s32[]{:T(128)}, bf16[4,128,512]{1,2,0:T(8,128)(2,1)S(1)}, s32[4,512]{1,0:T(4,128)S(1)}, bf16[128,4096]{1,0:T(8,128)(2,1)S(1)}, s32[]{:T(128)}) while((s32[]{:T(128)}, bf16[4,128,512]{1,2,0:T(8,128)(2,1)S(1)}, s32[4,512]{1,0:T(4,128)S(1)}, bf16[128,4096]{1,0:T(8,128)(2,1)S(1)}, s32[]{:T(128)}) %tuple.285), condition=%wide.region_20.21_spmd.clone, body=%wide.region_19.20_spmd.clone.sunk | while | flops 541130752 | bytes 1185861 | solution.py:35
  166.9 7.6 %while.162 = (s32[]{:T(128)}, bf16[4,128,512]{1,2,0:T(8,128)(2,1)S(1)}, s32[4,512]{1,0:T(4,128)S(1)}, bf16[128,2048]{1,0:T(8,128)(2,1)}, s32[]{:T(128)}) while((s32[]{:T(128)}, bf16[4,128,512]{1,2,0:T(8,128)(2,1)S(1)}, s32[4,512]{1,0:T(4,128)S(1)}, bf16[128,2048]{1,0:T(8,128)(2,1)}, s32[]{:T(128)}) %tuple.303), condition=%wide.region_22.23_spmd.clone, body=%wide.region_21.22_spmd.clone.sunk | while | flops 270598144 | bytes 661573 | solution.py:35
  167.0 1.9 fusion.408
  168.9 1.9 fusion.408
  170.8 1.9 fusion.408
  172.7 1.9 fusion.408
  175.4 3.4 %while.163 = (s32[]{:T(128)}, bf16[4,128,512]{1,2,0:T(8,128)(2,1)S(1)}, s32[4,512]{1,0:T(4,128)S(1)}, bf16[128,2048]{1,0:T(8,128)(2,1)S(1)}, s32[]{:T(128)}) while((s32[]{:T(128)}, bf16[4,128,512]{1,2,0:T(8,128)(2,1)S(1)}, s32[4,512]{1,0:T(4,128)S(1)}, bf16[128,2048]{1,0:T(8,128)(2,1)S(1)}, s32[]{:T(128)}) %tuple.310), condition=%wide.region_25.26_spmd.clone, body=%wide.region_24.25_spmd.clone.sunk | while | flops 270598144 | bytes 661573 | solution.py:35
  179.6 7.5 %while.164 = (s32[]{:T(128)}, bf16[4,128,512]{1,2,0:T(8,128)(2,1)S(1)}, s32[4,512]{1,0:T(4,128)S(1)}, bf16[128,2048]{1,0:T(8,128)(2,1)}, s32[]{:T(128)}) while((s32[]{:T(128)}, bf16[4,128,512]{1,2,0:T(8,128)(2,1)S(1)}, s32[4,512]{1,0:T(4,128)S(1)}, bf16[128,2048]{1,0:T(8,128)(2,1)}, s32[]{:T(128)}) %tuple.291), condition=%wide.region_28.29_spmd.clone, body=%wide.region_27.28_spmd.clone.sunk | while | flops 270598144 | bytes 661573 | solution.py:35
  179.6 1.9 fusion.414
  181.5 1.9 fusion.414
  183.3 1.9 fusion.414
  185.2 1.9 fusion.414
  187.9 3.4 %while.165 = (s32[]{:T(128)}, bf16[4,128,512]{1,2,0:T(8,128)(2,1)S(1)}, s32[4,512]{1,0:T(4,128)S(1)}, bf16[128,2048]{1,0:T(8,128)(2,1)S(1)}, s32[]{:T(128)}) while((s32[]{:T(128)}, bf16[4,128,512]{1,2,0:T(8,128)(2,1)S(1)}, s32[4,512]{1,0:T(4,128)S(1)}, bf16[128,2048]{1,0:T(8,128)(2,1)S(1)}, s32[]{:T(128)}) %tuple.308), condition=%wide.region_31.32_spmd.clone, body=%wide.region_30.31_spmd.clone.sunk | while | flops 270598144 | bytes 661573 | solution.py:35
  192.1 3.4 %while.166 = (s32[]{:T(128)}, bf16[4,128,512]{1,2,0:T(8,128)(2,1)S(1)}, s32[4,512]{1,0:T(4,128)S(1)}, bf16[128,2048]{1,0:T(8,128)(2,1)S(1)}, s32[]{:T(128)}) while((s32[]{:T(128)}, bf16[4,128,512]{1,2,0:T(8,128)(2,1)S(1)}, s32[4,512]{1,0:T(4,128)S(1)}, bf16[128,2048]{1,0:T(8,128)(2,1)S(1)}, s32[]{:T(128)}) %tuple.309), condition=%wide.region_34.35_spmd.clone, body=%wide.region_33.34_spmd.clone.sunk | while | flops 270598144 | bytes 661573 | solution.py:35
  196.3 7.9 %while.167 = (s32[]{:T(128)}, bf16[4,128,512]{1,2,0:T(8,128)(2,1)S(1)}, s32[4,512]{1,0:T(4,128)S(1)}, bf16[128,2048]{1,0:T(8,128)(2,1)}, s32[]{:T(128)}) while((s32[]{:T(128)}, bf16[4,128,512]{1,2,0:T(8,128)(2,1)S(1)}, s32[4,512]{1,0:T(4,128)S(1)}, bf16[128,2048]{1,0:T(8,128)(2,1)}, s32[]{:T(128)}) %tuple.311), condition=%wide.region_37.38_spmd.clone, body=%wide.region_36.37_spmd.clone.sunk | while | flops 270598144 | bytes 661573 | solution.py:35
  196.3 1.9 fusion.423
  198.3 1.9 fusion.423
  200.2 1.9 fusion.423
  202.0 1.9 fusion.423
  204.1 2.2 fusion.230
  206.3 1.6 convolution_add_fusion.7
  207.9 1.7 convolution_add_fusion.6
  210.8 1.5 fusion.229
  212.3 1.7 convolution_add_fusion.4
  214.0 1.6 convolution_add_fusion.3
  216.7 1.5 fusion.228
  218.2 1.5 convolution_add_fusion.1
  221.7 23.2 %reduce-scatter.2.cloned.1.call-done = f32[3,128,128]{1,2,0:T(8,128)} async-done(((f32[3,512,128]{1,2,0:T(8,128)}), f32[3,128,128]{1,2,0:T(8,128)}) %reduce-scatter.2.cloned.1.call-update) | async-done | bytes 196624 | tf_op jit(solution)/shard_map/reduce_scatter | solution.py:114
  (257 shorter events, 80.9 us)
Async XLA Ops:
  9.4 12.3 %copy-start.15 = (s32[3,2048,1]{1,2,0:T(1,128)S(1)}, s32[3,2048,1]{1,2,0:T(1,128)}, u32[]{:S(2)}) copy-start(s32[3,2048,1]{1,2,0:T(1,128)} %param.37) | copy-start | bytes 73732
  9.4 12.3 %copy-start.1 = (bf16[3,128,2048]{2,1,0:T(8,128)(2,1)S(1)}, bf16[3,128,2048]{2,1,0:T(8,128)(2,1)}, u32[]{:S(2)}) copy-start(bf16[3,128,2048]{2,1,0:T(8,128)(2,1)} %param.35) | copy-start | bytes 4718596
  14.4 20.1 %all-to-all-start = ((s32[8,1,512]{2,1,0:T(1,128)}), s32[8,1,512]{2,1,0:T(1,128)S(1)}, u32[]{:S(2)}, u32[]{:S(2)}) async-start(s32[8,1,512]{2,1,0:T(1,128)} %copy.32), calls=%async_computation | async-start | bytes 32768 | tf_op jit(solution)/shard_map/all_to_all | solution.py:83
  21.8 1.0 copy-start.18
  21.8 1.7 copy-start.16
  21.8 11.2 %copy-start.17 = (s32[8,2048]{1,0:T(8,128)S(1)}, s32[8,2048]{1,0:T(8,128)}, u32[]{:S(2)}) copy-start(s32[8,2048]{1,0:T(8,128)} %param.39) | copy-start | bytes 196612
  34.5 18.2 %all-to-all-start.2 = ((s32[8,1,512]{2,1,0:T(1,128)}), s32[8,1,512]{2,1,0:T(1,128)S(1)}, u32[]{:S(2)}, u32[]{:S(2)}) async-start(s32[8,1,512]{2,1,0:T(1,128)} %copy.35), calls=%async_computation.2 | async-start | bytes 32768 | tf_op jit(solution)/shard_map/all_to_all | solution.py:83
  52.7 16.9 %all-to-all-start.4 = ((s32[8,1,512]{2,1,0:T(1,128)}), s32[8,1,512]{2,1,0:T(1,128)S(1)}, u32[]{:S(2)}, u32[]{:S(2)}) async-start(s32[8,1,512]{2,1,0:T(1,128)} %copy.38), calls=%async_computation.4 | async-start | bytes 32768 | tf_op jit(solution)/shard_map/all_to_all | solution.py:83
  69.6 30.3 %all-to-all-start.1 = ((bf16[8,128,1,512]{1,3,2,0:T(8,128)(2,1)}), bf16[8,128,1,512]{1,3,2,0:T(8,128)(2,1)S(1)}, u32[]{:S(2)}, u32[]{:S(2)}) async-start(bf16[8,128,1,512]{1,3,2,0:T(8,128)(2,1)} %fusion.274), calls=%async_computation.1 | async-start | bytes 2097152 | tf_op jit(solution)/shard_map/all_to_all | solution.py:15
  99.9 29.2 %all-to-all-start.3 = ((bf16[8,128,1,512]{1,3,2,0:T(8,128)(2,1)}), bf16[8,128,1,512]{1,3,2,0:T(8,128)(2,1)S(1)}, u32[]{:S(2)}, u32[]{:S(2)}) async-start(bf16[8,128,1,512]{1,3,2,0:T(8,128)(2,1)} %fusion.266), calls=%async_computation.3 | async-start | bytes 2097152 | tf_op jit(solution)/shard_map/all_to_all | solution.py:15
  129.1 1.0 copy-start
  130.1 29.5 %all-to-all-start.5 = ((bf16[8,128,1,512]{1,3,2,0:T(8,128)(2,1)}), bf16[8,128,1,512]{1,3,2,0:T(8,128)(2,1)S(1)}, u32[]{:S(2)}, u32[]{:S(2)}) async-start(bf16[8,128,1,512]{1,3,2,0:T(8,128)(2,1)} %fusion.258), calls=%async_computation.5 | async-start | bytes 2097152 | tf_op jit(solution)/shard_map/all_to_all | solution.py:15
  133.7 111.2 %reduce-scatter.2.cloned.1.call-start = ((), (), s32[]{:S(2)}) async-start(), calls=%async_computation.7 | async-start | bytes 983040 | tf_op jit(solution)/shard_map/reduce_scatter | solution.py:114
  148.7 1.1 copy-start.2
  157.4 2.2 copy-start.4
  166.9 7.7 %copy-start.14 = (bf16[128,2048]{1,0:T(8,128)(2,1)S(1)}, bf16[128,2048]{1,0:T(8,128)(2,1)}, u32[]{:S(2)}) copy-start(bf16[128,2048]{1,0:T(8,128)(2,1)} %get-tuple-element.1258) | copy-start | bytes 1572868
  174.6 0.8 copy-start.6
  178.8 0.8 copy-start.7
  178.9 8.4 %copy-start.13 = (bf16[128,2048]{1,0:T(8,128)(2,1)S(1)}, bf16[128,2048]{1,0:T(8,128)(2,1)}, u32[]{:S(2)}) copy-start(bf16[128,2048]{1,0:T(8,128)(2,1)} %get-tuple-element.1256) | copy-start | bytes 1572868
  187.1 0.8 copy-start.9
  191.3 0.8 copy-start.10
  195.5 0.8 copy-start.11
  196.3 7.9 %copy-start.3 = (bf16[4,128,512]{1,2,0:T(8,128)(2,1)S(1)}, bf16[4,128,512]{1,2,0:T(8,128)(2,1)}, u32[]{:S(2)}) copy-start(bf16[4,128,512]{1,2,0:T(8,128)(2,1)} %copy-done.2) | copy-start | bytes 1572868
  196.3 10.1 %copy-start.5 = (bf16[4,128,512]{1,2,0:T(8,128)(2,1)S(1)}, bf16[4,128,512]{1,2,0:T(8,128)(2,1)}, u32[]{:S(2)}) copy-start(bf16[4,128,512]{1,2,0:T(8,128)(2,1)} %copy-done.4) | copy-start | bytes 1572868
  206.3 4.4 %copy-start.23 = (f32[128]{0:T(128)S(1)}, f32[128]{0:T(128)}, u32[]{:S(2)}) copy-start(f32[128]{0:T(128)} %broadcast_maximum_fusion.4) | copy-start | bytes 1540
  207.9 2.8 %copy-start.8 = (bf16[4,128,512]{1,2,0:T(8,128)(2,1)S(1)}, bf16[4,128,512]{1,2,0:T(8,128)(2,1)}, u32[]{:S(2)}) copy-start(bf16[4,128,512]{1,2,0:T(8,128)(2,1)} %copy-done.7) | copy-start | bytes 1572868
  207.9 4.3 %copy-start.22 = (f32[128]{0:T(128)S(1)}, f32[128]{0:T(128)}, u32[]{:S(2)}) copy-start(f32[128]{0:T(128)} %broadcast_maximum_fusion.3) | copy-start | bytes 1540
  209.6 4.3 %copy-start.21 = (f32[128]{0:T(128)S(1)}, f32[128]{0:T(128)}, u32[]{:S(2)}) copy-start(f32[128]{0:T(128)} %broadcast_maximum_fusion.2) | copy-start | bytes 1540
  212.2 4.5 %copy-start.12 = (bf16[4,128,512]{1,2,0:T(8,128)(2,1)S(1)}, bf16[4,128,512]{1,2,0:T(8,128)(2,1)}, u32[]{:S(2)}) copy-start(bf16[4,128,512]{1,2,0:T(8,128)(2,1)} %copy-done.11) | copy-start | bytes 1572868
  212.2 4.5 %copy-start.20 = (f32[128]{0:T(128)S(1)}, f32[128]{0:T(128)}, u32[]{:S(2)}) copy-start(f32[128]{0:T(128)} %broadcast_maximum_fusion.1) | copy-start | bytes 1540
  214.0 4.2 %copy-start.19 = (f32[128]{0:T(128)S(1)}, f32[128]{0:T(128)}, u32[]{:S(2)}) copy-start(f32[128]{0:T(128)} %broadcast_maximum_fusion) | copy-start | bytes 1540
Sparse Core Ops, SparseCore 0:
  221.9 22.9 reduce-scatter.1
